TPU v7x, 256 devices: a whole 4x4x8 slice. The times are simulated.
256 devices in a mesh: dp: 16 (over x, z_lo), owner: 16 (over z_hi, y, core).
Axes of the slice: x: 4, y: 4, z: 8 (z_hi: 2, z_lo: 4; z = z_hi * 4 + z_lo), core: 2. Of those that a mesh axis runs over, the one named last changes fastest.
Arguments:
- layer_input: bfloat16 [4096, 8192], P('dp', 'owner'), may hold values from -6 to 6
- output_grads: bfloat16 [4096, 10240], P('dp', 'owner'), may hold values from -6 to 6
- projection: bfloat16 [8192, 10240], P('owner', 'dp'), may hold values from -0.0625 to 0.0625
Outputs:
- grad_input: bfloat16 [4096, 8192], P('dp', 'owner')
- update_query: bfloat16 [8192, 8192], P('owner', 'dp')
- update_kv: bfloat16 [8192, 2048], P('owner', 'dp')
All inputs are finite; a program needn't handle non-finite values.
Results may differ from a plain program's by a relative error of at most 0.023.
Values may be sent and summed in bfloat16 or wider, within the bound.
A program may use at most 128 MiB of HBM per device.

v0:
```python
import math
import jax
import jax.numpy as jnp
from jax import lax
from jax.sharding import Mesh
from jax.sharding import PartitionSpec as P

BLOCK = 512
QW = 8192
DP = ("dp_0", "dp_1")


def gather_axes(shard, axes, dim):
    whole = shard
    for number in range(len(axes) - 1, -1, -1):
        whole = lax.all_gather(whole, axes[number], axis=dim, tiled=True)
    return whole


def split_up(shard, dim, devices):
    before, after = (shard.shape[:dim], shard.shape[dim + 1 :])
    return jnp.moveaxis(shard.reshape(*before, devices, -1, *after), dim, 0)


def sum_at_owner(shard, axis, dim):
    devices = lax.axis_size(axis)
    blocks = lax.all_to_all(split_up(shard, dim, devices), axis, 0, 0, tiled=True)
    return jnp.sum(blocks.astype(jnp.float32), axis=0)


def left_stat(blocks):
    return jnp.einsum("...ij,...kj->...ik", blocks, blocks, preferred_element_type=jnp.float32)


def right_stat(blocks):
    return jnp.einsum("...ji,...jk->...ik", blocks, blocks, preferred_element_type=jnp.float32)


def inverse_root(statistic):
    width = statistic.shape[-1]
    scale = math.sqrt(width) * jnp.sqrt(
        jnp.mean(statistic * statistic, axis=(-2, -1), keepdims=True) + 1e-06
    )
    normed = statistic / scale
    identity = jnp.eye(width, dtype=jnp.float32)
    return scale ** (-0.25) * (5.0 * identity - normed) * 0.25


def left_finish(square, received):
    width = square.shape[-1]
    root_left = inverse_root(left_stat(square))
    whole = jnp.einsum("...ij,...jk->...ik", root_left, received, precision=lax.Precision.HIGHEST)
    return (whole * math.sqrt(width)).astype(jnp.bfloat16)


def precondition(blocks):
    root_right = inverse_root(right_stat(blocks))
    half = jnp.einsum(
        "...ij,...jk->...ik",
        blocks.astype(jnp.float32),
        root_right,
        precision=lax.Precision.HIGHEST,
    )
    return left_finish(blocks, half)


def place_block(buffer, result, row_start, col_start):
    return lax.dynamic_update_slice(buffer, result, (row_start, col_start))


def body(layer_input, output_grads, projection):
    width = BLOCK
    rows_own = layer_input.shape[1]
    gathered = lax.all_gather(output_grads, "owner", axis=1, tiled=True)
    section = gathered
    input_sum = jnp.einsum(
        "tc,rc->tr", section, gather_axes(projection, DP, 1), preferred_element_type=jnp.float32
    )
    grad_input = input_sum.astype(jnp.bfloat16)
    section = lax.slice_in_dim(gathered, 0, QW // lax.axis_size(DP) * lax.axis_size(DP), axis=1)
    query_local = lax.psum_scatter(
        jnp.einsum("tc,tr->cr", section, layer_input, preferred_element_type=jnp.float32).astype(
            jnp.bfloat16
        ),
        DP,
        scatter_dimension=0,
        tiled=True,
    )
    query_count = query_local.shape[0] // width
    row_count = rows_own // width
    shaped = query_local.reshape(query_count, width, row_count, width)
    squares = jnp.transpose(shaped, (2, 0, 3, 1)).reshape(row_count * query_count, width, width)
    updates = precondition(squares)
    update_query = jnp.transpose(
        updates.reshape(row_count, query_count, width, width), (0, 2, 1, 3)
    ).reshape(rows_own, query_count * width)
    kv_term = jnp.einsum(
        "tc,tr->cr", gathered[:, QW:], layer_input, preferred_element_type=jnp.float32
    )
    kv_grads = lax.psum(kv_term.astype(jnp.bfloat16), DP)
    kv_count = kv_grads.shape[0] // width
    total = row_count * kv_count
    index_dp = lax.axis_index(DP)
    buffer = jnp.zeros((rows_own, kv_grads.shape[0]), jnp.float32)
    empty_square = jnp.zeros((width, width), jnp.float32)
    number = 0 + index_dp
    valid = number < total
    clamped = jnp.minimum(number, total - 1)
    block_row = clamped // kv_count
    block_col = clamped % kv_count
    square = lax.dynamic_slice(kv_grads, (block_col * width, block_row * width), (width, width)).T
    square, row_start, col_start = (square, block_row * width, block_col * width)
    result = lax.cond(
        valid,
        lambda operand: precondition(operand).astype(jnp.float32),
        lambda operand: empty_square,
        square,
    )
    buffer = place_block(buffer, result, row_start, col_start)
    update_kv = sum_at_owner(buffer.astype(jnp.bfloat16), DP, 1).astype(jnp.bfloat16)
    return (grad_input, update_query, update_kv)


def solution(mesh):
    torus = Mesh(mesh.devices.reshape(4, 4, mesh.shape["owner"]), ("dp_0", "dp_1", "owner"))
    placed = (P(DP, "owner"), P(DP, "owner"), P("owner", DP))
    return jax.shard_map(
        body,
        mesh=torus,
        in_specs=placed,
        out_specs=(P(DP, "owner"), P("owner", DP), P("owner", DP)),
        check_vma=False,
    )
```

profile of v0, /device:TPU:1, one launch (start us, length us, event | category | flops | bytes accessed | tf_op | source)
XLA Modules:
  0.0 656.7 jit_solution(5530023113139257753)
XLA Ops:
  7.2 0.0 copy-start
  7.2 0.0 all-gather.4.cloned.1.call-start
  7.2 0.7 all-gather.4.cloned.1.call-update
  7.9 0.0 all-gather.6.cloned.1.call-start
  8.0 0.7 all-gather.6.cloned.1.call-update
  8.7 0.0 all-reduce.2.cloned.1.call-start
  8.7 91.2 %all-gather.4.cloned.1.call-done = bf16[256,10240]{1,0:T(8,128)(2,1)} async-done(((bf16[256,640]{1,0:T(8,128)(2,1)}), bf16[256,10240]{1,0:T(8,128)(2,1)}) %all-gather.4.cloned.1.call-update) | async-done | bytes 5242896 | tf_op jit(solution)/shard_map/all_gather | solution.py:74
  99.9 0.0 copy-done
  99.9 3.4 convolution_convert_fusion.1
  103.3 0.0 all-reduce.2.cloned.1.call-update
  103.3 0.0 all-gather.8.cloned.1.call-start
  103.4 51.8 %all-gather.6.cloned.1.call-done = bf16[512,2560]{1,0:T(8,128)(2,1)} async-done(((bf16[512,640]{1,0:T(8,128)(2,1)}), bf16[512,2560]{1,0:T(8,128)(2,1)}) %all-gather.6.cloned.1.call-update) | async-done | bytes 2621456 | tf_op jit(solution)/shard_map/all_gather | solution.py:16
  155.2 0.0 all-gather.8.cloned.1.call-update
  155.2 0.0 reduce-scatter.2.cloned.1.call-start
  155.2 7.9 %convolution_convert_fusion = bf16[8192,512]{1,0:T(8,128)(2,1)} fusion(bf16[256,512]{1,0:T(8,128)(2,1)S(1)} %copy-done, bf16[256,10240]{1,0:T(8,128)(2,1)} %all-gather.4.cloned.1.call-done), kind=kOutput, calls=%fused_computation.31 | convolution fusion | flops 2151677952 | bytes 12845056 | tf_op jit(solution)/shard_map/tc,tr->cr/dot_general | solution.py:82
  163.1 0.0 reduce-scatter.2.cloned.1.call-update
  163.2 161.2 %all-reduce.2.cloned.1.call-done = bf16[2048,512]{1,0:T(8,128)(2,1)} async-done(((bf16[2048,512]{1,0:T(8,128)(2,1)}), bf16[2048,512]{1,0:T(8,128)(2,1)}) %all-reduce.2.cloned.1.call-update) | async-done | bytes 2097168 | tf_op jit(solution)/shard_map/psum | solution.py:100
  324.4 1.1 dynamic-slice_bitcast_fusion
  325.5 7.2 %conditional.1 = (bf16[512,512]{0,1:T(8,128)(2,1)S(1)}) conditional(s32[]{:T(128)} %convert_element_type.36, () %tuple.14, bf16[512,512]{0,1:T(8,128)(2,1)S(1)} %dynamic-slice_bitcast_fusion), branch_computations={%region_4.5_spmd, %region_5.8_spmd} | conditional | flops 3762814976 | bytes 9437328 | solution.py:113
  325.5 1.2 multiply_reduce_fusion
  327.4 1.1 fusion.7
  328.5 1.2 multiply_reduce_fusion.1
  330.4 2.0 fusion.1
  332.4 0.2 copy.13
  332.7 0.1 broadcast_in_dim.4
  332.9 2.4 copy.10
  335.3 50.0 %all_to_all.5 = bf16[16,512,128]{2,1,0:T(8,128)(2,1)S(1)} all-to-all(bf16[16,512,128]{2,1,0:T(8,128)(2,1)} %copy.10), channel_id=1, replica_groups=mesh['dp_0'=4,'dp_1'=4,'owner'=16] {'dp_0','dp_1'}, dimensions={0} | all-to-all | bytes 4194304 | tf_op jit(solution)/shard_map/all_to_all | solution.py:27
  385.3 1.0 reduce_sum.50
  386.2 65.5 %all-gather.8.cloned.1.call-done = bf16[512,10240]{1,0:T(8,128)(2,1)} async-done(((bf16[512,2560]{1,0:T(8,128)(2,1)}), bf16[512,10240]{1,0:T(8,128)(2,1)}) %all-gather.8.cloned.1.call-update) | async-done | bytes 10485776 | tf_op jit(solution)/shard_map/all_gather | solution.py:16
  451.7 9.2 %convolution_convert_fusion.2 = bf16[256,512]{1,0:T(8,128)(2,1)} fusion(bf16[256,10240]{1,0:T(8,128)(2,1)} %all-gather.4.cloned.1.call-done, bf16[512,10240]{1,0:T(8,128)(2,1)} %all-gather.8.cloned.1.call-done), kind=kOutput, calls=%fused_computation.38 | convolution fusion | flops 2684485632 | bytes 15990784 | tf_op jit(solution)/shard_map/tc,rc->tr/dot_general | solution.py:76
  460.9 178.0 %reduce-scatter.2.cloned.1.call-done = bf16[512,512]{1,0:T(8,128)(2,1)} async-done(((bf16[8192,512]{1,0:T(8,128)(2,1)}), bf16[512,512]{1,0:T(8,128)(2,1)}) %reduce-scatter.2.cloned.1.call-update) | async-done | bytes 524304 | tf_op jit(solution)/shard_map/reduce_scatter | solution.py:81
  638.8 2.4 multiply_reduce_fusion.2
  641.9 2.4 multiply_reduce_fusion.3
  645.2 2.3 fusion.34
  647.4 2.8 fusion.28
  (1 shorter events, 0.0 us)
Async XLA Ops:
  7.2 92.8 %copy-start = (bf16[256,512]{1,0:T(8,128)(2,1)S(1)}, bf16[256,512]{1,0:T(8,128)(2,1)}, u32[]{:S(2)}) copy-start(bf16[256,512]{1,0:T(8,128)(2,1)} %param.5) | copy-start | bytes 786436
  7.2 92.8 %all-gather.4.cloned.1.call-start = ((), (), s32[]{:S(2)}) async-start(), calls=%async_computation.2 | async-start | bytes 5570560 | tf_op jit(solution)/shard_map/all_gather | solution.py:74
  7.9 147.2 %all-gather.6.cloned.1.call-start = ((), (), s32[]{:S(2)}) async-start(), calls=%async_computation.3 | async-start | bytes 3276800 | tf_op jit(solution)/shard_map/all_gather | solution.py:16
  8.7 315.7 %all-reduce.2.cloned.1.call-start = ((), (), s32[]{:S(2)}) async-start(), calls=%async_computation.6 | async-start | bytes 4194304 | tf_op jit(solution)/shard_map/psum | solution.py:100
  103.3 348.4 %all-gather.8.cloned.1.call-start = ((), (), s32[]{:S(2)}) async-start(), calls=%async_computation.4 | async-start | bytes 13107200 | tf_op jit(solution)/shard_map/all_gather | solution.py:16
  155.2 483.7 %reduce-scatter.2.cloned.1.call-start = ((), (), s32[]{:S(2)}) async-start(), calls=%async_computation.5 | async-start | bytes 8912896 | tf_op jit(solution)/shard_map/reduce_scatter | solution.py:81
Sparse Core Ops, SparseCore 0:
  10.7 89.1 all-gather.3
  101.8 53.3 all-gather.5
  157.8 166.5 all-reduce.1
  326.0 125.6 all-gather.7
  454.1 184.6 reduce-scatter.1
where the time goes:
time: 657 us
  waiting for transfers between devices  549 us (84%)
  blocking collectives  50 us (8%)
  matrix products  35.8 us (5%)
  between operations  15.3 us (2%)
    reduce_scatter x1, waiting for transfers between devices, body(): lax.psum_scatter(jnp.einsum('tc,tr->cr', section, layer_input, preferred_...  178 us
    psum x1, waiting for transfers between devices, body(): kv_grads = lax.psum(kv_term.astype(jnp.bfloat16), DP)  161 us
    all_gather x2, waiting for transfers between devices, gather_axes(): whole = lax.all_gather(whole, axes[number], axis=dim, tiled=True)  117 us
    all_gather x1, waiting for transfers between devices, body(): gathered = lax.all_gather(output_grads, 'owner', axis=1, tiled=True)  91.2 us
    all_to_all x1, blocking collectives, sum_at_owner(): lax.all_to_all(split_up(shard, dim, devices), axis, 0, 0, tiled=True)  50 us
  transfers between devices with their start and end apart: 5, of which 5 were waited for; matrix products, arithmetic and copies ran while one was open for 5% of the time, Pallas kernels for 0%

commit v1 on v0

--- a/solution.py
+++ b/solution.py
@@ -97,7 +97,7 @@
     kv_term = jnp.einsum(
         "tc,tr->cr", gathered[:, QW:], layer_input, preferred_element_type=jnp.float32
     )
-    kv_grads = lax.psum(kv_term.astype(jnp.bfloat16), DP)
+    kv_grads = lax.psum(lax.psum(kv_term.astype(jnp.bfloat16), "dp_0"), "dp_1")
     kv_count = kv_grads.shape[0] // width
     total = row_count * kv_count
     index_dp = lax.axis_index(DP)

time: 657 us -> 509 us (0.77)
  waiting for transfers between devices: 549 us -> 351 us
  blocking collectives: 50 us -> 97.9 us
    all_gather x2, waiting for transfers between devices: 117 us -> 0.03 us  [gather_axes(): whole = lax.all_gather(whole, axes[number], axis=dim, tiled=True)]
    reduce_scatter x1, waiting for transfers between devices: 178 us -> 111 us  [body(): lax.psum_scatter(jnp.einsum('tc,tr->cr', section, layer_input, preferred_...]
    all_to_all x1, blocking collectives: 50 us -> 97.9 us  [sum_at_owner(): lax.all_to_all(split_up(shard, dim, devices), axis, 0, 0, tiled=True)]
    psum x1 -> x2, waiting for transfers between devices: 161 us -> 146 us  [body(): kv_grads = lax.psum(lax.psum(kv_term.astype(jnp.bfloat16), 'dp_0'), 'dp_1')]
  transfers between devices with their start and end apart: 5 -> 6, of which waited for: 5 -> 4; matrix products, arithmetic and copies ran while one was open for 5% -> 5% of each run, Pallas kernels for 0% -> 0%
where the time goes in v1:
time: 509 us; the launch traced here: 508 us
  waiting for transfers between devices  351 us (69%)
  blocking collectives  97.9 us (19%)
  matrix products  35.8 us (7%)
  between operations  16.8 us (3%)
    psum x2, waiting for transfers between devices, body(): kv_grads = lax.psum(lax.psum(kv_term.astype(jnp.bfloat16), 'dp_0'), 'dp_1')  146 us
    reduce_scatter x1, waiting for transfers between devices, body(): lax.psum_scatter(jnp.einsum('tc,tr->cr', section, layer_input, preferred_...  111 us
    all_to_all x1, blocking collectives, sum_at_owner(): lax.all_to_all(split_up(shard, dim, devices), axis, 0, 0, tiled=True)  97.9 us
    all_gather x1, waiting for transfers between devices, body(): gathered = lax.all_gather(output_grads, 'owner', axis=1, tiled=True)  92 us
  transfers between devices with their start and end apart: 6, of which 4 were waited for; matrix products, arithmetic and copies ran while one was open for 5% of the time, Pallas kernels for 0%

profile of v1, /device:TPU:1, one launch (start us, length us, event | category | flops | bytes accessed | tf_op | source)
XLA Modules:
  0.0 508.1 jit_solution(14772399127779316900)
XLA Ops:
  8.0 0.0 copy-start
  8.0 0.0 all-gather.4.cloned.1.call-start
  8.1 0.7 all-gather.4.cloned.1.call-update
  8.7 0.0 all-reduce.3.cloned.1.call-start
  8.8 92.0 %all-gather.4.cloned.1.call-done = bf16[256,10240]{1,0:T(8,128)(2,1)} async-done(((bf16[256,640]{1,0:T(8,128)(2,1)}), bf16[256,10240]{1,0:T(8,128)(2,1)}) %all-gather.4.cloned.1.call-update) | async-done | bytes 5242896 | tf_op jit(solution)/shard_map/all_gather | solution.py:74
  100.8 0.0 copy-done
  100.8 3.3 convolution_convert_fusion.1
  104.1 0.0 all-reduce.3.cloned.1.call-update
  104.1 0.0 all-gather.6.cloned.1.call-start
  104.2 0.5 all-gather.6.cloned.1.call-update
  104.7 0.0 all-reduce.5.cloned.1.call-start
  104.7 58.2 %all-reduce.3.cloned.1.call-done = bf16[2048,512]{1,0:T(8,128)(2,1)} async-done(((bf16[2048,512]{1,0:T(8,128)(2,1)}), bf16[2048,512]{1,0:T(8,128)(2,1)}) %all-reduce.3.cloned.1.call-update) | async-done | bytes 2097168 | tf_op jit(solution)/shard_map/psum | solution.py:100
  162.9 0.0 all-reduce.5.cloned.1.call-update
  163.0 0.0 all-gather.8.cloned.1.call-start
  163.0 0.0 all-gather.6.cloned.1.call-done
  163.1 0.6 all-gather.8.cloned.1.call-update
  163.7 0.0 reduce-scatter.2.cloned.1.call-start
  163.8 7.9 %convolution_convert_fusion = bf16[8192,512]{1,0:T(8,128)(2,1)} fusion(bf16[256,512]{1,0:T(8,128)(2,1)S(1)} %copy-done, bf16[256,10240]{1,0:T(8,128)(2,1)} %all-gather.4.cloned.1.call-done), kind=kOutput, calls=%fused_computation.31 | convolution fusion | flops 2151677952 | bytes 12845056 | tf_op jit(solution)/shard_map/tc,tr->cr/dot_general | solution.py:82
  171.7 0.0 reduce-scatter.2.cloned.1.call-update
  171.7 88.0 %all-reduce.5.cloned.1.call-done = bf16[2048,512]{1,0:T(8,128)(2,1)} async-done(((bf16[2048,512]{1,0:T(8,128)(2,1)}), bf16[2048,512]{1,0:T(8,128)(2,1)}) %all-reduce.5.cloned.1.call-update) | async-done | bytes 2097168 | tf_op jit(solution)/shard_map/psum | solution.py:100
  259.7 1.1 dynamic-slice_bitcast_fusion
  260.8 7.2 %conditional.1 = (bf16[512,512]{0,1:T(8,128)(2,1)S(1)}) conditional(s32[]{:T(128)} %convert_element_type.36, () %tuple.14, bf16[512,512]{0,1:T(8,128)(2,1)S(1)} %dynamic-slice_bitcast_fusion), branch_computations={%region_5.6_spmd, %region_6.9_spmd} | conditional | flops 3762814976 | bytes 9437328 | solution.py:113
  260.8 1.2 multiply_reduce_fusion
  262.7 1.1 fusion.7
  263.8 1.2 multiply_reduce_fusion.1
  265.8 2.0 fusion.1
  267.8 0.2 copy.13
  268.0 0.1 broadcast_in_dim.4
  268.2 2.4 copy.10
  270.6 97.9 %all_to_all.5 = bf16[16,512,128]{2,1,0:T(8,128)(2,1)S(1)} all-to-all(bf16[16,512,128]{2,1,0:T(8,128)(2,1)} %copy.10), channel_id=1, replica_groups=mesh['dp_0'=4,'dp_1'=4,'owner'=16] {'dp_0','dp_1'}, dimensions={0} | all-to-all | bytes 4194304 | tf_op jit(solution)/shard_map/all_to_all | solution.py:27
  368.5 1.0 reduce_sum.50
  369.5 0.0 all-gather.8.cloned.1.call-done
  369.5 9.3 %convolution_convert_fusion.2 = bf16[256,512]{1,0:T(8,128)(2,1)} fusion(bf16[256,10240]{1,0:T(8,128)(2,1)} %all-gather.4.cloned.1.call-done, bf16[512,10240]{1,0:T(8,128)(2,1)} %all-gather.8.cloned.1.call-done), kind=kOutput, calls=%fused_computation.38 | convolution fusion | flops 2684485632 | bytes 15990784 | tf_op jit(solution)/shard_map/tc,rc->tr/dot_general | solution.py:76
  378.7 110.8 %reduce-scatter.2.cloned.1.call-done = bf16[512,512]{1,0:T(8,128)(2,1)} async-done(((bf16[8192,512]{1,0:T(8,128)(2,1)}), bf16[512,512]{1,0:T(8,128)(2,1)}) %reduce-scatter.2.cloned.1.call-update) | async-done | bytes 524304 | tf_op jit(solution)/shard_map/reduce_scatter | solution.py:81
  489.6 2.4 multiply_reduce_fusion.2
  492.7 2.4 multiply_reduce_fusion.3
  495.9 2.3 fusion.34
  498.2 2.8 fusion.28
  (1 shorter events, 0.0 us)
Async XLA Ops:
  8.0 92.8 %copy-start = (bf16[256,512]{1,0:T(8,128)(2,1)S(1)}, bf16[256,512]{1,0:T(8,128)(2,1)}, u32[]{:S(2)}) copy-start(bf16[256,512]{1,0:T(8,128)(2,1)} %param.5) | copy-start | bytes 786436
  8.0 92.8 %all-gather.4.cloned.1.call-start = ((), (), s32[]{:S(2)}) async-start(), calls=%async_computation.2 | async-start | bytes 5570560 | tf_op jit(solution)/shard_map/all_gather | solution.py:74
  8.7 154.2 %all-reduce.3.cloned.1.call-start = ((), (), s32[]{:S(2)}) async-start(), calls=%async_computation.6 | async-start | bytes 4194304 | tf_op jit(solution)/shard_map/psum | solution.py:100
  104.1 58.9 %all-gather.6.cloned.1.call-start = ((), (), s32[]{:S(2)}) async-start(), calls=%async_computation.3 | async-start | bytes 3276800 | tf_op jit(solution)/shard_map/all_gather | solution.py:16
  104.7 155.0 %all-reduce.5.cloned.1.call-start = ((), (), s32[]{:S(2)}) async-start(), calls=%async_computation.7 | async-start | bytes 4194304 | tf_op jit(solution)/shard_map/psum | solution.py:100
  163.0 206.5 %all-gather.8.cloned.1.call-start = ((), (), s32[]{:S(2)}) async-start(), calls=%async_computation.4 | async-start | bytes 13107200 | tf_op jit(solution)/shard_map/all_gather | solution.py:16
  163.7 325.9 %reduce-scatter.2.cloned.1.call-start = ((), (), s32[]{:S(2)}) async-start(), calls=%async_computation.5 | async-start | bytes 8912896 | tf_op jit(solution)/shard_map/reduce_scatter | solution.py:81
Sparse Core Ops, SparseCore 0:
  11.6 89.1 all-gather.3
  104.2 58.6 all-reduce.2
  165.6 103.1 all-gather.7
  271.2 218.3 reduce-scatter.1
Sparse Core Ops, SparseCore 1:
  106.4 53.1 all-gather.5
  163.1 96.6 all-reduce.4
